TPU v7x, 256 devices: a whole 4x4x8 slice. The times are simulated.
256 devices in a mesh: seq: 64 (over y, z_lo, x), tp: 4 (over z_hi, core).
Axes of the slice: x: 4, y: 4, z: 8 (z_hi: 2, z_lo: 4; z = z_hi * 4 + z_lo), core: 2. Of those that a mesh axis runs over, the one named last changes fastest.
Arguments:
- hidden_in: bfloat16 [16384, 4096], P('seq', 'tp'), may hold values from -6 to 6
- order: int32 [16384], P('seq'), may hold values from 0 to 16383, as said below
- segment: int32 [16384], replicated, may hold values from 0 to 31, never falling along the last dimension, each value on 1 to 2048 neighbouring positions
- norm_gain: float32 [4096], replicated, may hold values from 0.1 to 1.9
- w_query: bfloat16 [4096, 2048], P('seq', 'tp')
- w_key: bfloat16 [4096, 512], P('seq', 'tp'), may hold values from -0.09375 to 0.09375
- w_value: bfloat16 [4096, 512], P('seq', 'tp'), may hold values from -0.09375 to 0.09375
- w_out: bfloat16 [2048, 4096], P('seq', 'tp'), may hold values from -0.5 to 0.5
Outputs:
- attn_out: bfloat16 [16384, 4096], P('seq', 'tp')
Inputs may be any that keep to these rules, and one draw needn't show every extreme that they name: order holds every position once; it is made of runs of 64 consecutive positions, each starting at a multiple of 64 and stored in rows that start at a multiple of 64. `segment`: never falls along positions.
All inputs are finite; a program needn't handle non-finite values.
Results may differ from a plain program's by a relative error of at most 0.014.
The roundings to bfloat16 on the way count: a program that leaves them out, or rounds other values in their place, can miss the bound.
Values may be sent and summed in bfloat16 or wider, within the bound.
No kernel may reach another device: no remote copies, remote signals or barrier semaphores. Data moves between devices by JAX's collectives and lax.ppermute only.
A program may use at most 128 MiB of HBM per device.

v0:
```python
import jax
import jax.numpy as jnp
from jax import lax
from jax.sharding import Mesh
from jax.sharding import PartitionSpec as P

HD = 128
SEQ = ("seq_0", "seq_1", "seq_2")
THETA = 500000.0
EPS = 1e-05


def sent_to_all(array, axis):
    copies = jnp.broadcast_to(array, (lax.axis_size(axis), *array.shape))
    return lax.all_to_all(copies, axis, split_axis=0, concat_axis=0, tiled=True)


def joined_along(blocks, dim):
    blocks = jnp.moveaxis(blocks, 0, dim)
    dims = blocks.shape
    return blocks.reshape(*dims[:dim], dims[dim] * dims[dim + 1], *dims[dim + 2 :])


def gather_directly(array, axis, dim):
    blocks = sent_to_all(array, axis)
    return joined_along(blocks, dim)


def side_by_side(arrays, axis, dim, along):
    widths = [a.shape[along] for a in arrays]
    both = jnp.concatenate(arrays, axis=along)
    filled = lax.all_gather(both, axis, axis=dim, tiled=True)
    return tuple(jnp.split(filled, [sum(widths[:k]) for k in range(1, len(widths))], axis=along))


def stacked_from(array, axes, sequence):
    blocks = array
    for k in sequence:
        blocks = lax.all_gather(blocks, axes[k])
    done = sequence[::-1]
    back = [done.index(k) for k in range(len(axes))]
    blocks = blocks.transpose(*back, *range(len(axes), blocks.ndim))
    return blocks.reshape(-1, *array.shape)


def gathered_by_axis(array, axes, sequence, dim):
    return joined_along(stacked_from(array, axes, sequence), dim)


def rotary(block, positions):
    head_dim = block.shape[-1]
    width = head_dim // 2
    frequency = THETA ** (-jnp.arange(width, dtype=jnp.float32) * 2.0 / head_dim)
    angle = positions.astype(jnp.float32)[:, None] * frequency[None, :]
    cosine = jnp.cos(angle)[:, None, :]
    sine = jnp.sin(angle)[:, None, :]
    first = block[..., :width]
    second = block[..., width:]
    return jnp.concatenate(
        [first * cosine - second * sine, second * cosine + first * sine], axis=-1
    )


def on_device(hidden_in, order, segment, norm_gain, w_query, w_key, w_value, w_out):
    rows = hidden_in.shape[0]
    whole = gather_directly(hidden_in, "tp", 1)
    wide = whole.astype(jnp.float32)
    mean_square = jnp.mean(wide * wide, axis=1, keepdims=True)
    normed = (wide * lax.rsqrt(mean_square + EPS) * norm_gain[None, :]).astype(jnp.bfloat16)
    pieces = side_by_side((w_query, w_key, w_value), SEQ, 0, 1)
    columns = normed
    query, key, value = tuple(
        (jnp.dot(columns, piece, preferred_element_type=jnp.float32) for piece in pieces)
    )
    heads_local = w_query.shape[1] // HD
    groups_local = w_key.shape[1] // HD
    group = heads_local // groups_local
    query = (rotary(query.reshape(rows, heads_local, HD), order) * HD ** (-0.5)).astype(
        jnp.bfloat16
    )
    query = query.reshape(rows, groups_local, group, HD)
    key = rotary(key.reshape(rows, groups_local, HD), order).astype(jnp.bfloat16)
    value = value.reshape(rows, groups_local, HD).astype(jnp.bfloat16)
    document = jnp.take(segment, order, axis=0)

    def attend(carry, block):
        key_block, value_block, key_order, key_document = block
        allowed = (key_order[None, :] <= order[:, None]) & (
            key_document[None, :] == document[:, None]
        )
        maximum, total, weighted = carry
        scores = jnp.einsum("rkgd,ckd->rkgc", query, key_block, preferred_element_type=jnp.float32)
        scores = jnp.where(allowed[:, None, None, :], scores, -jnp.inf)
        new_max = jnp.maximum(maximum, jnp.max(scores, axis=-1))
        anchor = jnp.where(new_max == -jnp.inf, 0.0, new_max)
        weights = jnp.exp(scores - anchor[..., None])
        shrink = jnp.exp(maximum - anchor)
        total = total * shrink + jnp.sum(weights, axis=-1)
        weighted = weighted * shrink[..., None] + jnp.einsum(
            "rkgc,ckd->rkgd",
            weights.astype(jnp.bfloat16),
            value_block,
            preferred_element_type=jnp.float32,
        )
        return (new_max, total, weighted)

    initial = (
        jnp.full((rows, groups_local, group), -jnp.inf, jnp.float32),
        jnp.zeros((rows, groups_local, group), jnp.float32),
        jnp.zeros((rows, groups_local, group, HD), jnp.float32),
    )
    carry = initial
    piece = (
        *side_by_side((key, value), SEQ, 0, 1),
        lax.all_gather(order, SEQ, axis=0, tiled=True),
        lax.all_gather(document, SEQ, axis=0, tiled=True),
    )
    count = piece[0].shape[0]
    stacked = tuple((member.reshape((count // 512, 512) + member.shape[1:]) for member in piece))
    carry, unused = lax.scan(lambda state, block: (attend(state, block), None), carry, stacked)
    maximum, total, weighted = carry
    mixed = (weighted / total[..., None]).reshape(rows, heads_local * HD).astype(jnp.bfloat16)
    every_head = gather_directly(mixed, "tp", 1)
    piece = gathered_by_axis(w_out, SEQ, (1, 0, 2), 0)
    columns = every_head
    result = jnp.dot(columns, piece, preferred_element_type=jnp.float32)
    return result.astype(jnp.bfloat16)


def solution(mesh):
    torus = Mesh(mesh.devices.reshape(4, 4, 4, mesh.shape["tp"]), ("seq_0", "seq_1", "seq_2", "tp"))
    placed = (
        P(SEQ, "tp"),
        P(SEQ),
        P(),
        P(),
        P(SEQ, "tp"),
        P(SEQ, "tp"),
        P(SEQ, "tp"),
        P(SEQ, "tp"),
    )
    return jax.shard_map(
        on_device, mesh=torus, in_specs=placed, out_specs=P(SEQ, "tp"), check_vma=False
    )
```

profile of v0, /device:TPU:1, one launch (start us, length us, event | category | flops | bytes accessed | tf_op | source)
XLA Modules:
  0.0 937.8 jit_solution(4467411417672132659)
XLA Ops:
  8.1 2.6 broadcast_in_dim.58
  10.8 9.9 %all-to-all-start = ((bf16[4,256,1024]{2,1,0:T(8,128)(2,1)}), bf16[4,256,1024]{2,1,0:T(8,128)(2,1)}, u32[]{:S(2)}, u32[]{:S(2)}) async-start(bf16[4,256,1024]{2,1,0:T(8,128)(2,1)} %broadcast_in_dim.58), calls=%async_computation | async-start | bytes 4194304 | tf_op jit(solution)/shard_map/all_to_all | solution.py:15
  20.7 67.4 %all-gather = bf16[128,1024]{1,0:T(8,128)(2,1)} all-gather(bf16[32,1024]{1,0:T(8,128)(2,1)S(1)} %copy-done.5), channel_id=2, replica_groups=mesh['seq_0'=4,'seq_1'=4,'seq_2'=4,'tp'=4] {'seq_1'}, dimensions={0}, use_global_device_ids=true | all-gather | bytes 327680 | tf_op jit(solution)/shard_map/all_gather | solution.py:39
  88.3 1.7 gather_fusion
  90.0 2.9 copy.37
  93.5 1.7 fusion.21
  95.2 248.8 %all-gather.10.cloned.1.call-done = bf16[4096,768]{1,0:T(8,128)(2,1)} async-done(((bf16[64,768]{1,0:T(8,128)(2,1)}), bf16[4096,768]{1,0:T(8,128)(2,1)}) %all-gather.10.cloned.1.call-update) | async-done | bytes 6291472 | tf_op jit(solution)/shard_map/all_gather | solution.py:32
  344.0 2.4 convolution_bitcast_fusion.1
  346.7 2.4 fusion.22
  349.9 159.7 %all-gather.4 = s32[64,1,256]{2,1,0:T(1,128)S(1)} all-gather(s32[1,1,256]{2,1,0:T(1,128)S(1)} %bitcast.141), channel_id=1, replica_groups=mesh['seq_0'=4,'seq_1'=4,'seq_2'=4,'tp'=4] {'seq_0','seq_1','seq_2'}, dimensions={0}, use_global_device_ids=true | all-gather | bytes 66560 | tf_op jit(solution)/shard_map/all_gather | solution.py:116
  509.8 155.2 %all-gather.3 = s32[64,1,256]{2,1,0:T(1,128)S(1)} all-gather(s32[1,1,256]{2,1,0:T(1,128)S(1)} %bitcast.140), channel_id=1, replica_groups=mesh['seq_0'=4,'seq_1'=4,'seq_2'=4,'tp'=4] {'seq_0','seq_1','seq_2'}, dimensions={0}, use_global_device_ids=true | all-gather | bytes 66560 | tf_op jit(solution)/shard_map/all_gather | solution.py:115
  665.6 1.7 multiply_convert_fusion
  667.3 4.5 slice_bitcast_fusion
  671.8 6.6 copy.39
  678.4 3.4 fusion.36
  682.2 5.1 fusion.34
  687.3 2.5 copy.52
  689.8 6.4 copy.48
  696.2 117.0 %while.15 = (s32[]{:T(128)}, f32[256,1,4]{0,2,1:T(4,128)S(1)}, f32[256,1,4]{0,2,1:T(4,128)S(1)}, f32[256,1,4,128]{0,3,2,1:T(8,128)S(1)}, s32[32,512]{1,0:T(8,128...) while((s32[]{:T(128)}, f32[256,1,4]{0,2,1:T(4,128)S(1)}, ...), condition=%wide.region_4.5_spmd.clone, body=%wide.region_1.4_spmd.clone.sunk | while | flops 273428480 | bytes 8476829 | solution.py:120
  764.1 1.6 fusion.56
  814.4 95.3 %all-to-all-start.1 = ((bf16[4,256,512]{1,2,0:T(8,128)(2,1)}), bf16[4,256,512]{1,2,0:T(8,128)(2,1)S(1)}, u32[]{:S(2)}, u32[]{:S(2)}) async-start(bf16[4,256,512]{1,2,0:T(8,128)(2,1)} %broadcast_in_dim.59), calls=%async_computation.1 | async-start | bytes 2097152 | tf_op jit(solution)/shard_map/all_to_all | solution.py:15
  909.7 5.0 copy.44
  914.7 12.4 %all-to-all-done.1 = bf16[4,256,512]{1,2,0:T(8,128)(2,1)S(1)} async-done(((bf16[4,256,512]{1,2,0:T(8,128)(2,1)}), bf16[4,256,512]{1,2,0:T(8,128)(2,1)S(1)}, u32[]{:S(2)}, u32[]{:S(2)}) %all-to-all-start.1) | async-done | bytes 1048608 | tf_op jit(solution)/shard_map/all_to_all | solution.py:15
  927.0 4.3 convolution_convert_fusion
  (334 shorter events, 118.7 us)
Async XLA Ops:
  6.5 81.7 %copy-start = (s32[16384]{0:T(1024)S(1)}, s32[16384]{0:T(1024)}, u32[]{:S(2)}) copy-start(s32[16384]{0:T(1024)} %param.12) | copy-start | bytes 196612
  6.5 14.2 %copy-start.5 = (bf16[32,1024]{1,0:T(8,128)(2,1)S(1)}, bf16[32,1024]{1,0:T(8,128)(2,1)}, u32[]{:S(2)}) copy-start(bf16[32,1024]{1,0:T(8,128)(2,1)} %param.17) | copy-start | bytes 196612
  6.5 81.7 %copy-start.3 = (s32[256]{0:T(256)S(1)}, s32[256]{0:T(256)}, u32[]{:S(2)}) copy-start(s32[256]{0:T(256)} %param.11) | copy-start | bytes 3076
  6.5 337.4 %all-gather.10.cloned.1.call-start = ((), (), s32[]{:S(2)}) async-start(), calls=%async_computation.2 | async-start | bytes 6389760 | tf_op jit(solution)/shard_map/all_gather | solution.py:32
  10.8 79.2 %all-to-all-start = ((bf16[4,256,1024]{2,1,0:T(8,128)(2,1)}), bf16[4,256,1024]{2,1,0:T(8,128)(2,1)}, u32[]{:S(2)}, u32[]{:S(2)}) async-start(bf16[4,256,1024]{2,1,0:T(8,128)(2,1)} %broadcast_in_dim.58), calls=%async_computation | async-start | bytes 4194304 | tf_op jit(solution)/shard_map/all_to_all | solution.py:15
  20.7 72.8 %copy-start.4 = (f32[4096]{0:T(1024)S(1)}, f32[4096]{0:T(1024)}, u32[]{:S(2)}) copy-start(f32[4096]{0:T(1024)} %param.13) | copy-start | bytes 49156
  20.7 644.9 %all-gather.14.cloned.1.call-start = ((), (), s32[]{:S(2)}) async-start(), calls=%async_computation.4 | async-start | bytes 1310720 | tf_op jit(solution)/shard_map/all_gather | solution.py:39
  88.2 594.0 %all-gather.12.cloned.1.call-start = ((), (), s32[]{:S(2)}) async-start(), calls=%async_computation.3 | async-start | bytes 8519680 | tf_op jit(solution)/shard_map/all_gather | solution.py:32
  349.8 559.8 %all-gather.16.cloned.1.call-start = ((), (), s32[]{:S(2)}) async-start(), calls=%async_computation.5 | async-start | bytes 5242880 | tf_op jit(solution)/shard_map/all_gather | solution.py:39
  671.8 6.6 copy-start.2
  814.4 112.7 %all-to-all-start.1 = ((bf16[4,256,512]{1,2,0:T(8,128)(2,1)}), bf16[4,256,512]{1,2,0:T(8,128)(2,1)S(1)}, u32[]{:S(2)}, u32[]{:S(2)}) async-start(bf16[4,256,512]{1,2,0:T(8,128)(2,1)} %broadcast_in_dim.59), calls=%async_computation.1 | async-start | bytes 2097152 | tf_op jit(solution)/shard_map/all_to_all | solution.py:15
  909.7 21.6 %copy-start.1 = (s32[16384]{0:T(1024)S(1)}, s32[16384]{0:T(1024)}, u32[]{:S(2)}) copy-start(s32[16384]{0:T(1024)} %param.12) | copy-start | bytes 196612
Sparse Core Ops, SparseCore 0:
  9.1 334.8 all-gather.9
  345.8 63.5 all-gather.13
  411.1 267.4 all-gather.11
  680.2 121.1 all-gather.15
where the time goes:
time: 940 us; the launch traced here: 938 us
  blocking collectives  382 us (41%)
  waiting for transfers between devices  261 us (28%)
  matrix products  106 us (11%)
  starting transfers between devices  105 us (11%)
  local copies, waits for them, and re-layouts  39.1 us (4%)
  other arithmetic  27.8 us (3%)
  between operations  13.3 us (1%)
    all_gather x2, waiting for transfers between devices, side_by_side(): filled = lax.all_gather(both, axis, axis=dim, tiled=True)  249 us
    all_gather x1, blocking collectives, on_device(): lax.all_gather(document, SEQ, axis=0, tiled=True)  160 us
    all_gather x1, blocking collectives, on_device(): lax.all_gather(order, SEQ, axis=0, tiled=True)  155 us
    all_to_all x2, starting transfers between devices, sent_to_all(): return lax.all_to_all(copies, axis, split_axis=0, concat_axis=0, tiled=True)  105 us
    all_gather x1, blocking collectives, stacked_from(): blocks = lax.all_gather(blocks, axes[k])  67.4 us
    dot_general x32, matrix products, attend(): jnp.einsum('rkgc,ckd->rkgd', weights.astype(jnp.bfloat16), value_block, p...  50.5 us
    dot_general x32, matrix products, attend(): jnp.einsum('rkgd,ckd->rkgc', query, key_block, preferred_element_type=jnp...  43.4 us
  transfers between devices with their start and end apart: 6, of which 2 were waited for; matrix products, arithmetic and copies ran while one was open for 18% of the time, Pallas kernels for 0%

commit v1 on v0

--- a/solution.py
+++ b/solution.py
@@ -113,7 +113,9 @@
     piece = (
         *side_by_side((key, value), SEQ, 0, 1),
         lax.all_gather(order, SEQ, axis=0, tiled=True),
-        lax.all_gather(document, SEQ, axis=0, tiled=True),
+        jnp.concatenate(
+            lax.all_to_all(jnp.stack([document] * lax.axis_size(SEQ)), SEQ, 0, 0), axis=0
+        ),
     )
     count = piece[0].shape[0]
     stacked = tuple((member.reshape((count // 512, 512) + member.shape[1:]) for member in piece))

time: 940 us -> 886 us (0.943)
  blocking collectives: 382 us -> 228 us
  waiting for transfers between devices: 261 us -> 411 us
  starting transfers between devices: 105 us -> 55.6 us
    all_gather x1 -> x0, blocking collectives: 160 us -> none  [on_device(): lax.all_gather(document, SEQ, axis=0, tiled=True)]
    all_gather x2, waiting for transfers between devices: 249 us -> 391 us  [side_by_side(): filled = lax.all_gather(both, axis, axis=dim, tiled=True)]
    all_to_all x2, starting transfers between devices: 105 us -> 47.3 us  [sent_to_all(): return lax.all_to_all(copies, axis, split_axis=0, concat_axis=0, tiled=True)]
  transfers between devices with their start and end apart: 6 -> 7, of which waited for: 2 -> 3; matrix products, arithmetic and copies ran while one was open for 18% -> 19% of each run, Pallas kernels for 0% -> 0%
where the time goes in v1:
time: 886 us; the launch traced here: 884 us
  waiting for transfers between devices  411 us (46%)
  blocking collectives  228 us (26%)
  matrix products  106 us (12%)
  starting transfers between devices  55.6 us (6%)
  local copies, waits for them, and re-layouts  39.7 us (4%)
  other arithmetic  27.8 us (3%)
  between operations  13.4 us (2%)
    all_gather x2, waiting for transfers between devices, side_by_side(): filled = lax.all_gather(both, axis, axis=dim, tiled=True)  391 us
    all_gather x1, blocking collectives, on_device(): lax.all_gather(order, SEQ, axis=0, tiled=True)  161 us
    all_gather x1, blocking collectives, stacked_from(): blocks = lax.all_gather(blocks, axes[k])  67.4 us
    dot_general x32, matrix products, attend(): jnp.einsum('rkgc,ckd->rkgd', weights.astype(jnp.bfloat16), value_block, p...  50.5 us
    all_to_all x2, starting transfers between devices, sent_to_all(): return lax.all_to_all(copies, axis, split_axis=0, concat_axis=0, tiled=True)  47.3 us
    dot_general x32, matrix products, attend(): jnp.einsum('rkgd,ckd->rkgc', query, key_block, preferred_element_type=jnp...  43.4 us
    all_to_all x2, waiting for transfers between devices, sent_to_all(): return lax.all_to_all(copies, axis, split_axis=0, concat_axis=0, tiled=True)  19.2 us
  transfers between devices with their start and end apart: 7, of which 3 were waited for; matrix products, arithmetic and copies ran while one was open for 19% of the time, Pallas kernels for 0%

profile of v1, /device:TPU:1, one launch (start us, length us, event | category | flops | bytes accessed | tf_op | source)
XLA Modules:
  0.0 883.7 jit_solution(508804764846708839)
XLA Ops:
  8.1 2.6 broadcast_in_dim.58
  10.8 9.9 %all-to-all-start.1 = ((bf16[4,256,1024]{2,1,0:T(8,128)(2,1)}), bf16[4,256,1024]{2,1,0:T(8,128)(2,1)}, u32[]{:S(2)}, u32[]{:S(2)}) async-start(bf16[4,256,1024]{2,1,0:T(8,128)(2,1)} %broadcast_in_dim.58), calls=%async_computation.1 | async-start | bytes 4194304 | tf_op jit(solution)/shard_map/all_to_all | solution.py:15
  20.7 67.4 %all-gather = bf16[128,1024]{1,0:T(8,128)(2,1)} all-gather(bf16[32,1024]{1,0:T(8,128)(2,1)S(1)} %copy-done.5), channel_id=2, replica_groups=mesh['seq_0'=4,'seq_1'=4,'seq_2'=4,'tp'=4] {'seq_1'}, dimensions={0}, use_global_device_ids=true | all-gather | bytes 327680 | tf_op jit(solution)/shard_map/all_gather | solution.py:39
  88.3 1.7 gather_fusion
  90.0 2.9 copy.37
  93.5 1.7 fusion.21
  95.2 248.7 %all-gather.9.cloned.1.call-done = bf16[4096,768]{1,0:T(8,128)(2,1)} async-done(((bf16[64,768]{1,0:T(8,128)(2,1)}), bf16[4096,768]{1,0:T(8,128)(2,1)}) %all-gather.9.cloned.1.call-update) | async-done | bytes 6291472 | tf_op jit(solution)/shard_map/all_gather | solution.py:32
  343.9 2.4 convolution_bitcast_fusion.1
  346.7 2.4 fusion.22
  350.5 8.3 all-to-all-start
  358.9 160.5 %all-gather.3 = s32[64,1,256]{2,1,0:T(1,128)S(1)} all-gather(s32[1,1,256]{2,1,0:T(1,128)S(1)} %bitcast.139), channel_id=1, replica_groups=mesh['seq_0'=4,'seq_1'=4,'seq_2'=4,'tp'=4] {'seq_0','seq_1','seq_2'}, dimensions={0}, use_global_device_ids=true | all-gather | bytes 66560 | tf_op jit(solution)/shard_map/all_gather | solution.py:115
  520.2 1.7 multiply_convert_fusion
  521.9 4.5 slice_bitcast_fusion
  526.4 6.5 copy.39
  532.9 3.5 fusion.36
  536.7 142.6 %all-gather.11.cloned.1.call-done = bf16[16384,2,128]{0,2,1:T(8,128)(2,1)} async-done(((bf16[256,2,128]{0,2,1:T(8,128)(2,1)}), bf16[16384,2,128]{0,2,1:T(8,128)(2,1)}) %all-gather.11.cloned.1.call-update) | async-done | bytes 8388624 | tf_op jit(solution)/shard_map/all_gather | solution.py:32
  679.3 5.1 fusion.34
  684.4 2.5 copy.52
  686.9 6.4 copy.48
  693.3 117.1 %while.15 = (s32[]{:T(128)}, f32[256,1,4]{0,2,1:T(4,128)S(1)}, f32[256,1,4]{0,2,1:T(4,128)S(1)}, f32[256,1,4,128]{0,3,2,1:T(8,128)S(1)}, s32[32,512]{1,0:T(8,128...) while((s32[]{:T(128)}, f32[256,1,4]{0,2,1:T(4,128)S(1)}, ...), condition=%wide.region_4.5_spmd.clone, body=%wide.region_1.4_spmd.clone.sunk | while | flops 273428480 | bytes 8476829 | solution.py:122
  811.5 37.3 %all-to-all-start.2 = ((bf16[4,256,512]{1,2,0:T(8,128)(2,1)}), bf16[4,256,512]{1,2,0:T(8,128)(2,1)S(1)}, u32[]{:S(2)}, u32[]{:S(2)}) async-start(bf16[4,256,512]{1,2,0:T(8,128)(2,1)} %broadcast_in_dim.59), calls=%async_computation.2 | async-start | bytes 2097152 | tf_op jit(solution)/shard_map/all_to_all | solution.py:15
  848.8 5.0 copy.44
  853.8 19.2 %all-to-all-done.2 = bf16[4,256,512]{1,2,0:T(8,128)(2,1)S(1)} async-done(((bf16[4,256,512]{1,2,0:T(8,128)(2,1)}), bf16[4,256,512]{1,2,0:T(8,128)(2,1)S(1)}, u32[]{:S(2)}, u32[]{:S(2)}) %all-to-all-start.2) | async-done | bytes 1048608 | tf_op jit(solution)/shard_map/all_to_all | solution.py:15
  872.9 4.3 convolution_convert_fusion
  (336 shorter events, 121.0 us)
Async XLA Ops:
  6.5 81.7 %copy-start = (s32[16384]{0:T(1024)S(1)}, s32[16384]{0:T(1024)}, u32[]{:S(2)}) copy-start(s32[16384]{0:T(1024)} %param.12) | copy-start | bytes 196612
  6.5 14.2 %copy-start.5 = (bf16[32,1024]{1,0:T(8,128)(2,1)S(1)}, bf16[32,1024]{1,0:T(8,128)(2,1)}, u32[]{:S(2)}) copy-start(bf16[32,1024]{1,0:T(8,128)(2,1)} %param.17) | copy-start | bytes 196612
  6.5 81.7 %copy-start.3 = (s32[256]{0:T(256)S(1)}, s32[256]{0:T(256)}, u32[]{:S(2)}) copy-start(s32[256]{0:T(256)} %param.11) | copy-start | bytes 3076
  6.5 337.4 %all-gather.9.cloned.1.call-start = ((), (), s32[]{:S(2)}) async-start(), calls=%async_computation.3 | async-start | bytes 6389760 | tf_op jit(solution)/shard_map/all_gather | solution.py:32
  10.8 79.3 %all-to-all-start.1 = ((bf16[4,256,1024]{2,1,0:T(8,128)(2,1)}), bf16[4,256,1024]{2,1,0:T(8,128)(2,1)}, u32[]{:S(2)}, u32[]{:S(2)}) async-start(bf16[4,256,1024]{2,1,0:T(8,128)(2,1)} %broadcast_in_dim.58), calls=%async_computation.1 | async-start | bytes 4194304 | tf_op jit(solution)/shard_map/all_to_all | solution.py:15
  20.7 72.8 %copy-start.4 = (f32[4096]{0:T(1024)S(1)}, f32[4096]{0:T(1024)}, u32[]{:S(2)}) copy-start(f32[4096]{0:T(1024)} %param.13) | copy-start | bytes 49156
  20.7 499.4 %all-gather.13.cloned.1.call-start = ((), (), s32[]{:S(2)}) async-start(), calls=%async_computation.5 | async-start | bytes 1310720 | tf_op jit(solution)/shard_map/all_gather | solution.py:39
  88.2 591.1 %all-gather.11.cloned.1.call-start = ((), (), s32[]{:S(2)}) async-start(), calls=%async_computation.4 | async-start | bytes 8519680 | tf_op jit(solution)/shard_map/all_gather | solution.py:32
  350.5 169.4 %all-to-all-start = ((s32[64,1,256]{2,1,0:T(1,128)}), s32[64,1,256]{2,1,0:T(1,128)S(1)}, u32[]{:S(2)}, u32[]{:S(2)}) async-start(s32[64,1,256]{2,1,0:T(1,128)} %stack.2), calls=%async_computation | async-start | bytes 131072 | tf_op jit(solution)/shard_map/all_to_all | solution.py:117
  358.8 490.0 %all-gather.15.cloned.1.call-start = ((), (), s32[]{:S(2)}) async-start(), calls=%async_computation.6 | async-start | bytes 5242880 | tf_op jit(solution)/shard_map/all_gather | solution.py:39
  526.4 6.5 copy-start.2
  811.5 61.5 %all-to-all-start.2 = ((bf16[4,256,512]{1,2,0:T(8,128)(2,1)}), bf16[4,256,512]{1,2,0:T(8,128)(2,1)S(1)}, u32[]{:S(2)}, u32[]{:S(2)}) async-start(bf16[4,256,512]{1,2,0:T(8,128)(2,1)} %broadcast_in_dim.59), calls=%async_computation.2 | async-start | bytes 2097152 | tf_op jit(solution)/shard_map/all_to_all | solution.py:15
  848.8 28.4 %copy-start.1 = (s32[16384]{0:T(1024)S(1)}, s32[16384]{0:T(1024)}, u32[]{:S(2)}) copy-start(s32[16384]{0:T(1024)} %param.12) | copy-start | bytes 196612
Sparse Core Ops, SparseCore 0:
  9.1 334.7 all-gather.8
  345.7 63.8 all-gather.12
  411.4 267.9 all-gather.10
  681.0 80.5 all-gather.14
